TPU v7x, 32 devices: a whole 2x2x4 slice. The times are simulated.
32 devices in a mesh: dp: 16 (over z, y, x), mp: 2 (over core).
Axes of the slice: x: 2, y: 2, z: 4, core: 2. Of those that a mesh axis runs over, the one named last changes fastest.
Arguments:
- embeddings: float32 [12288, 1024], P('dp', 'mp')
- cluster_id: int32 [12288], P('dp'), may hold values from 0 to 4095, as said below
- centroids: float32 [4096, 1024], P('dp', 'mp'), may hold values from -6 to 6
- cluster_mass: float32 [4096], P('dp'), may hold values from 1 to 16
Outputs:
- max_similarity: float32 [12288], P('dp')
- new_centroids: float32 [4096, 1024], P('dp', 'mp')
Inputs may be any that keep to these rules, and one draw needn't show every extreme that they name: `cluster_id`: cluster k belongs to owner k // 256. Among the 768 rows of one index of dp, at most 96 have clusters of any one owner, and for some owner exactly 96.
All inputs are finite; a program needn't handle non-finite values.
Results may differ from a plain program's by a relative error of at most 0.0011.
Values may be sent and summed in bfloat16 or wider, within the bound.
No kernel may reach another device: no remote copies, remote signals or barrier semaphores. Data moves between devices by JAX's collectives and lax.ppermute only.
A program may use at most 64 MiB of HBM per device.

v0:
```python
import jax
import jax.numpy as jnp
from jax import lax
from jax.sharding import PartitionSpec as P

D = 1024


def shards(embeddings, cluster_id, centroids, cluster_mass):
    owners = lax.axis_size("dp")
    row_count = embeddings.shape[0]
    slot_count = 2 * row_count
    capacity = slot_count // owners
    cluster_count = centroids.shape[0]
    squares = lax.psum(jnp.sum(embeddings * embeddings, axis=1), "mp")
    unit = (embeddings * lax.rsqrt(squares / D + 1e-06)[:, None]).astype(jnp.bfloat16)
    owner = cluster_id // cluster_count
    local = cluster_id - owner * cluster_count
    owner_hot = (owner[:, None] == jnp.arange(owners, dtype=jnp.int32)[None, :]).astype(
        jnp.bfloat16
    )
    row_index = jnp.arange(row_count, dtype=jnp.int32)
    lower = (row_index[:, None] >= row_index[None, :]).astype(jnp.bfloat16)
    running = jnp.dot(lower, owner_hot, preferred_element_type=jnp.float32)
    rank = jnp.sum(running * owner_hot.astype(jnp.float32), axis=1).astype(jnp.int32) - 1
    slot = owner * capacity + rank
    slot_index = jnp.arange(slot_count, dtype=jnp.int32)
    placed = slot_index[:, None] == slot[None, :]
    outgoing = jnp.dot(
        placed.astype(jnp.bfloat16), unit, preferred_element_type=jnp.float32
    ).astype(jnp.bfloat16)
    out_ids = jnp.max(jnp.where(placed, local[None, :] + 1, 0), axis=1) - 1
    incoming, in_ids = (
        lax.all_to_all(outgoing, "dp", split_axis=0, concat_axis=0, tiled=True),
        lax.all_to_all(out_ids, "dp", split_axis=0, concat_axis=0, tiled=True),
    )
    member = (jnp.arange(cluster_count, dtype=jnp.int32)[:, None] == in_ids[None, :]).astype(
        jnp.bfloat16
    )
    sums = jnp.dot(member, incoming, preferred_element_type=jnp.float32)
    counts = jnp.sum(member.astype(jnp.float32), axis=1)
    new_centroids = (cluster_mass[:, None] * centroids + sums) / (cluster_mass + counts)[:, None]
    half = slot_count // lax.axis_size("mp")
    start = lax.axis_index("mp") * half
    contract = (((1,), (1,)), ((), ()))
    gathered = lax.all_gather(incoming, "mp", axis=1, tiled=True)
    queries = lax.dynamic_slice_in_dim(gathered, start, half, 0)
    scores = lax.dot_general(queries, gathered, contract, preferred_element_type=jnp.float32)
    scores = scores / D
    query_ids = lax.dynamic_slice_in_dim(in_ids, start, half, 0)
    query_pos = start + jnp.arange(half, dtype=jnp.int32)
    same = (
        (query_ids[:, None] == in_ids[None, :])
        & (query_ids[:, None] >= 0)
        & (query_pos[:, None] != slot_index[None, :])
    )
    best = jnp.max(jnp.where(same, scores, -1.0), axis=1)
    best_all = lax.all_gather(best, "mp", axis=0, tiled=True)
    returned = lax.all_to_all(best_all, "dp", split_axis=0, concat_axis=0, tiled=True)
    max_similarity = jnp.take(returned, slot)
    return (max_similarity, new_centroids)


def solution(mesh):
    in_specs = (P("dp", "mp"), P("dp"), P("dp", "mp"), P("dp"))
    out_specs = (P("dp"), P("dp", "mp"))
    return jax.shard_map(shards, mesh=mesh, in_specs=in_specs, out_specs=out_specs, check_vma=False)
```

profile of v0, /device:TPU:0, one launch (start us, length us, event | category | flops | bytes accessed | tf_op | source)
XLA Modules:
  0.0 107.2 jit_solution(10581560315133862556)
XLA Ops:
  7.2 0.0 copy-start.1
  7.2 0.0 all-gather.3.cloned.1.call-start
  7.2 0.8 add_select_fusion
  8.0 0.3 fusion.11
  8.4 0.7 compare_select_fusion
  9.1 1.6 %multiply_reduce_fusion = f32[768]{0:T(1024)S(1)} fusion(f32[768,512]{1,0:T(8,128)} %param.4), kind=kLoop, calls=%fused_computation.17 | loop fusion | flops 785664 | bytes 1575936 | tf_op jit(solution)/shard_map/reduce_sum | solution.py:15
  10.7 2.6 %psum.7 = f32[768]{0:T(1024)S(1)} all-reduce(f32[768]{0:T(1024)S(1)} %multiply_reduce_fusion), channel_id=1, replica_groups=mesh['dp'=16,'mp'=2] {'mp'}, use_global_device_ids=true, to_apply=%region_3.4 | all-reduce | flops 768 | bytes 6144 | tf_op jit(solution)/shard_map/psum | solution.py:15
  13.3 0.0 copy-done.1
  13.3 1.5 %fusion.2 = bf16[1536,512]{1,0:T(8,128)(2,1)S(1)} fusion(s32[768]{0:T(1024)S(1)} %get-tuple-element.3, f32[768,512]{1,0:T(8,128)S(1)} %copy-done.1, f32[768]{0:T(1024)S(1)} %add_rsqrt_fusion), kind=kOutput, calls=%fused_computation.7 | convolution fusion | flops 1210712064 | bytes 3151872 | tf_op jit(solution)/shard_map/dot_general | solution.py:29
  14.8 46.0 %all_to_all.33 = bf16[16,96,512]{2,1,0:T(8,128)(2,1)} all-to-all(bf16[16,96,512]{2,1,0:T(8,128)(2,1)S(1)} %bitcast.10), channel_id=1, replica_groups=mesh['dp'=16,'mp'=2] {'dp'}, dimensions={0} | all-to-all | bytes 3145728 | tf_op jit(solution)/shard_map/all_to_all | solution.py:34
  60.8 0.0 copy-start.2
  60.8 0.0 all-gather.3.cloned.1.call-update
  60.8 0.7 select_reduce_fusion.1
  61.5 0.7 sub.23
  62.2 3.9 %all-to-all-start = ((s32[16,96,1]{1,2,0:T(1,128)}), s32[16,96,1]{1,2,0:T(1,128)S(1)}, u32[]{:S(2)}, u32[]{:S(2)}) async-start(s32[16,96,1]{1,2,0:T(1,128)} %bitcast), calls=%async_computation | async-start | bytes 16384 | tf_op jit(solution)/shard_map/all_to_all | solution.py:35
  66.2 7.2 %all-to-all-done = s32[16,96,1]{1,2,0:T(1,128)S(1)} async-done(((s32[16,96,1]{1,2,0:T(1,128)}), s32[16,96,1]{1,2,0:T(1,128)S(1)}, u32[]{:S(2)}, u32[]{:S(2)}) %all-to-all-start) | async-done | bytes 6176 | tf_op jit(solution)/shard_map/all_to_all | solution.py:35
  73.4 0.5 broadcast.71
  73.9 0.7 reduce.7
  74.6 0.1 all_to_all.23
  74.6 0.2 convert_reduce_fusion
  74.9 0.0 copy-done.2
  74.9 0.1 broadcast_compare_fusion
  75.0 0.0 all-gather.3.cloned.1.call-done
  75.0 0.0 copy-start
  75.0 0.0 copy-start.3
  75.0 5.8 %select_reduce_fusion = f32[768]{0:T(1024)S(1)} fusion(bf16[1536,1024]{1,0:T(8,128)(2,1)} %all-gather.3.cloned.1.call-done, s32[768]{0:T(1024)S(1)} %iota_add_fusion, s32[1536]{0:T(1024)S(1)} %all_to_all.23, s32[768]{0:T(1024)S(1)} %get-tuple-element.5, pred[768]{0:T(1024)(128)(4,1)S(1)} %get-tuple-element.4, s32[]{:T(128)S(6)} %select_n.28), kind=kOutput, calls=%fused_computation.1 | convolution fusion | flops 2424175872 | bytes 4734724 | tf_op jit(solution)/shard_map/dot_general | solution.py:48
  80.8 1.8 %all-gather = f32[2,1,768]{2,1,0:T(1,128)S(1)} all-gather(f32[1,1,768]{2,1,0:T(1,128)S(1)} %reshape.52), channel_id=1, replica_groups=mesh['dp'=16,'mp'=2] {'mp'}, dimensions={0}, use_global_device_ids=true | all-gather | bytes 9216 | tf_op jit(solution)/shard_map/all_gather | solution.py:58
  82.6 0.7 all_to_all.27
  83.3 3.5 %all-to-all-start.2 = ((f32[16,96,1]{1,2,0:T(1,128)}), f32[16,96,1]{1,2,0:T(1,128)S(1)}, u32[]{:S(2)}, u32[]{:S(2)}) async-start(f32[16,96,1]{1,2,0:T(1,128)} %bitcast.3), calls=%async_computation.2 | async-start | bytes 16384 | tf_op jit(solution)/shard_map/all_to_all | solution.py:59
  86.8 0.0 copy-done
  86.8 0.0 copy-done.3
  86.8 1.4 %fusion.9 = f32[256,512]{1,0:T(8,128)} fusion(bf16[1536,512]{1,0:T(8,128)(2,1)S(1)} %bitcast.9, s32[1536]{0:T(1024)S(1)} %all_to_all.23, f32[256,512]{1,0:T(8,128)S(1)} %copy-done.3, f32[256]{0:T(256)S(1)} %add.65, f32[256]{0:T(256)S(1)} %copy-done.2), kind=kOutput, calls=%fused_computation.19 | convolution fusion | flops 403439616 | bytes 2629632 | tf_op jit(solution)/shard_map/dot_general | solution.py:40
  88.2 5.9 %all-to-all-done.2 = f32[16,96,1]{1,2,0:T(1,128)S(1)} async-done(((f32[16,96,1]{1,2,0:T(1,128)}), f32[16,96,1]{1,2,0:T(1,128)S(1)}, u32[]{:S(2)}, u32[]{:S(2)}) %all-to-all-start.2) | async-done | bytes 6176 | tf_op jit(solution)/shard_map/all_to_all | solution.py:59
  94.1 0.5 broadcast.72
  94.6 0.7 reduce.8
  95.3 0.1 all_to_all.29
  95.3 4.5 %gather_fusion = f32[768]{0:T(1024)S(1)} fusion(f32[1536]{0:T(1024)S(1)} %all_to_all.29, s32[1024]{0:T(1024)S(1)} %pad_clamp_fusion), kind=kCustom, calls=%fused_computation | custom fusion | bytes 9216 | tf_op jit(solution)/shard_map/jit(_take)/gather | solution.py:60
  99.8 0.6 and_select_fusion
  (7 shorter events, 0.1 us)
Async XLA Ops:
  7.2 6.2 %copy-start.1 = (f32[768,512]{1,0:T(8,128)S(1)}, f32[768,512]{1,0:T(8,128)}, u32[]{:S(2)}) copy-start(f32[768,512]{1,0:T(8,128)} %param.4) | copy-start | bytes 4718596
  7.2 67.8 %all-gather.3.cloned.1.call-start = ((), (), s32[]{:S(2)}) async-start(), calls=%async_computation.3 | async-start | bytes 4718592 | tf_op jit(solution)/shard_map/all_gather | solution.py:46
  60.8 14.1 %copy-start.2 = (f32[256]{0:T(256)S(1)}, f32[256]{0:T(256)}, u32[]{:S(2)}) copy-start(f32[256]{0:T(256)} %param.7) | copy-start | bytes 3076
  62.2 11.2 %all-to-all-start = ((s32[16,96,1]{1,2,0:T(1,128)}), s32[16,96,1]{1,2,0:T(1,128)S(1)}, u32[]{:S(2)}, u32[]{:S(2)}) async-start(s32[16,96,1]{1,2,0:T(1,128)} %bitcast), calls=%async_computation | async-start | bytes 16384 | tf_op jit(solution)/shard_map/all_to_all | solution.py:35
  75.0 11.8 %copy-start = (bf16[16,96,512]{2,1,0:T(8,128)(2,1)S(1)}, bf16[16,96,512]{2,1,0:T(8,128)(2,1)}, u32[]{:S(2)}) copy-start(bf16[16,96,512]{2,1,0:T(8,128)(2,1)} %all_to_all.33) | copy-start | bytes 4718596
  75.0 11.8 %copy-start.3 = (f32[256,512]{1,0:T(8,128)S(1)}, f32[256,512]{1,0:T(8,128)}, u32[]{:S(2)}) copy-start(f32[256,512]{1,0:T(8,128)} %param.6) | copy-start | bytes 1572868
  83.3 10.8 %all-to-all-start.2 = ((f32[16,96,1]{1,2,0:T(1,128)}), f32[16,96,1]{1,2,0:T(1,128)S(1)}, u32[]{:S(2)}, u32[]{:S(2)}) async-start(f32[16,96,1]{1,2,0:T(1,128)} %bitcast.3), calls=%async_computation.2 | async-start | bytes 16384 | tf_op jit(solution)/shard_map/all_to_all | solution.py:59
Sparse Core Ops, SparseCore 0:
  60.9 10.4 all-gather.2
where the time goes:
time: 108 us; the launch traced here: 107 us
  blocking collectives  50.4 us (47%)
  between operations  14.2 us (13%)
  waiting for transfers between devices  13.1 us (12%)
  matrix products  8.99 us (8%)
  starting transfers between devices  7.48 us (7%)
  local copies, waits for them, and re-layouts  6.99 us (6%)
  other arithmetic  6.12 us (6%)
    all_to_all x1, blocking collectives, shards(): lax.all_to_all(outgoing, 'dp', split_axis=0, concat_axis=0, tiled=True)  46 us
    all_to_all x1, waiting for transfers between devices, shards(): lax.all_to_all(out_ids, 'dp', split_axis=0, concat_axis=0, tiled=True)  7.2 us
    all_to_all x1, waiting for transfers between devices, shards(): lax.all_to_all(best_all, 'dp', split_axis=0, concat_axis=0, tiled=True)  5.86 us
    dot_general x1, matrix products, shards(): lax.dot_general(queries, gathered, contract, preferred_element_type=jnp.f...  5.79 us
    gather x1, local copies, waits for them, and re-layouts, shards(): max_similarity = jnp.take(returned, slot)  4.46 us
    all_to_all x1, starting transfers between devices, shards(): lax.all_to_all(out_ids, 'dp', split_axis=0, concat_axis=0, tiled=True)  3.95 us
    all_to_all x1, starting transfers between devices, shards(): lax.all_to_all(best_all, 'dp', split_axis=0, concat_axis=0, tiled=True)  3.49 us
    psum x1, blocking collectives, shards(): squares = lax.psum(jnp.sum(embeddings * embeddings, axis=1), 'mp')  2.63 us
  transfers between devices with their start and end apart: 3, of which 2 were waited for; matrix products, arithmetic and copies ran while one was open for 4% of the time, Pallas kernels for 0%

commit v1 on v0

--- a/solution.py
+++ b/solution.py
@@ -12,7 +12,7 @@
     slot_count = 2 * row_count
     capacity = slot_count // owners
     cluster_count = centroids.shape[0]
-    squares = lax.psum(jnp.sum(embeddings * embeddings, axis=1), "mp")
+    squares = jnp.sum(lax.all_gather(jnp.sum(embeddings * embeddings, axis=1), "mp"), axis=0)
     unit = (embeddings * lax.rsqrt(squares / D + 1e-06)[:, None]).astype(jnp.bfloat16)
     owner = cluster_id // cluster_count
     local = cluster_id - owner * cluster_count

time: 108 us -> 107 us (level)
    psum x1 -> x0, blocking collectives: 2.63 us -> none  [shards(): squares = lax.psum(jnp.sum(embeddings * embeddings, axis=1), 'mp')]
    all_gather x0 -> x1, blocking collectives: none -> 1.97 us  [shards(): lax.all_gather(jnp.sum(embeddings * embeddings, axis=1), 'mp')]
where the time goes in v1:
time: 107 us
  blocking collectives  49.8 us (47%)
  between operations  14.2 us (13%)
  waiting for transfers between devices  13.1 us (12%)
  matrix products  8.97 us (8%)
  starting transfers between devices  7.48 us (7%)
  local copies, waits for them, and re-layouts  7 us (7%)
  other arithmetic  6.13 us (6%)
    all_to_all x1, blocking collectives, shards(): lax.all_to_all(outgoing, 'dp', split_axis=0, concat_axis=0, tiled=True)  46 us
    all_to_all x1, waiting for transfers between devices, shards(): lax.all_to_all(out_ids, 'dp', split_axis=0, concat_axis=0, tiled=True)  7.2 us
    all_to_all x1, waiting for transfers between devices, shards(): lax.all_to_all(best_all, 'dp', split_axis=0, concat_axis=0, tiled=True)  5.86 us
    dot_general x1, matrix products, shards(): lax.dot_general(queries, gathered, contract, preferred_element_type=jnp.f...  5.78 us
    gather x1, local copies, waits for them, and re-layouts, shards(): max_similarity = jnp.take(returned, slot)  4.46 us
    all_to_all x1, starting transfers between devices, shards(): lax.all_to_all(out_ids, 'dp', split_axis=0, concat_axis=0, tiled=True)  3.95 us
    all_to_all x1, starting transfers between devices, shards(): lax.all_to_all(best_all, 'dp', split_axis=0, concat_axis=0, tiled=True)  3.49 us
  transfers between devices with their start and end apart: 3, of which 2 were waited for; matrix products, arithmetic and copies ran while one was open for 4% of the time, Pallas kernels for 0%

profile of v1, /device:TPU:0, one launch (start us, length us, event | category | flops | bytes accessed | tf_op | source)
XLA Modules:
  0.0 106.6 jit_solution(14323339533898512629)
XLA Ops:
  7.2 0.0 copy-start.1
  7.2 0.0 all-gather.5.cloned.1.call-start
  7.2 0.8 add_select_fusion
  8.0 0.3 fusion.11
  8.4 0.7 compare_select_fusion
  9.1 1.6 %multiply_reduce_fusion = f32[768]{0:T(1024)S(1)} fusion(f32[768,512]{1,0:T(8,128)} %param.4), kind=kLoop, calls=%fused_computation.17 | loop fusion | flops 785664 | bytes 1575936 | tf_op jit(solution)/shard_map/reduce_sum | solution.py:15
  10.7 2.0 %all-gather.1 = f32[2,1,768]{2,1,0:T(1,128)S(1)} all-gather(f32[1,1,768]{2,1,0:T(1,128)S(1)} %reshape.57), channel_id=2, replica_groups=mesh['dp'=16,'mp'=2] {'mp'}, dimensions={0}, use_global_device_ids=true | all-gather | bytes 9216 | tf_op jit(solution)/shard_map/all_gather | solution.py:15
  12.7 0.0 copy-done.1
  12.7 1.5 %fusion.2 = bf16[1536,512]{1,0:T(8,128)(2,1)S(1)} fusion(s32[768]{0:T(1024)S(1)} %get-tuple-element.3, f32[768,512]{1,0:T(8,128)S(1)} %copy-done.1, f32[768]{0:T(1024)S(1)} %add_rsqrt_fusion), kind=kOutput, calls=%fused_computation.7 | convolution fusion | flops 1210712064 | bytes 3151872 | tf_op jit(solution)/shard_map/dot_general | solution.py:29
  14.2 46.0 %all_to_all.33 = bf16[16,96,512]{2,1,0:T(8,128)(2,1)} all-to-all(bf16[16,96,512]{2,1,0:T(8,128)(2,1)S(1)} %bitcast.10), channel_id=1, replica_groups=mesh['dp'=16,'mp'=2] {'dp'}, dimensions={0} | all-to-all | bytes 3145728 | tf_op jit(solution)/shard_map/all_to_all | solution.py:34
  60.1 0.0 copy-start.2
  60.2 0.0 all-gather.5.cloned.1.call-update
  60.2 0.7 select_reduce_fusion.1
  60.9 0.7 sub.23
  61.6 3.9 %all-to-all-start = ((s32[16,96,1]{1,2,0:T(1,128)}), s32[16,96,1]{1,2,0:T(1,128)S(1)}, u32[]{:S(2)}, u32[]{:S(2)}) async-start(s32[16,96,1]{1,2,0:T(1,128)} %bitcast), calls=%async_computation | async-start | bytes 16384 | tf_op jit(solution)/shard_map/all_to_all | solution.py:35
  65.6 7.2 %all-to-all-done = s32[16,96,1]{1,2,0:T(1,128)S(1)} async-done(((s32[16,96,1]{1,2,0:T(1,128)}), s32[16,96,1]{1,2,0:T(1,128)S(1)}, u32[]{:S(2)}, u32[]{:S(2)}) %all-to-all-start) | async-done | bytes 6176 | tf_op jit(solution)/shard_map/all_to_all | solution.py:35
  72.7 0.5 broadcast.78
  73.3 0.7 reduce.8
  73.9 0.1 all_to_all.23
  74.0 0.2 convert_reduce_fusion
  74.2 0.0 copy-done.2
  74.3 0.1 broadcast_compare_fusion
  74.4 0.0 all-gather.5.cloned.1.call-done
  74.4 0.0 copy-start
  74.4 0.0 copy-start.3
  74.4 5.8 %select_reduce_fusion = f32[768]{0:T(1024)S(1)} fusion(bf16[1536,1024]{1,0:T(8,128)(2,1)} %all-gather.5.cloned.1.call-done, s32[768]{0:T(1024)S(1)} %iota_add_fusion, s32[1536]{0:T(1024)S(1)} %all_to_all.23, s32[768]{0:T(1024)S(1)} %get-tuple-element.5, pred[768]{0:T(1024)(128)(4,1)S(1)} %get-tuple-element.4, s32[]{:T(128)S(6)} %select_n.28), kind=kOutput, calls=%fused_computation.1 | convolution fusion | flops 2424175872 | bytes 4734724 | tf_op jit(solution)/shard_map/dot_general | solution.py:48
  80.2 1.8 %all-gather.2 = f32[2,1,768]{2,1,0:T(1,128)S(1)} all-gather(f32[1,1,768]{2,1,0:T(1,128)S(1)} %reshape.59), channel_id=1, replica_groups=mesh['dp'=16,'mp'=2] {'mp'}, dimensions={0}, use_global_device_ids=true | all-gather | bytes 9216 | tf_op jit(solution)/shard_map/all_gather | solution.py:58
  82.0 0.7 all_to_all.27
  82.7 3.5 %all-to-all-start.2 = ((f32[16,96,1]{1,2,0:T(1,128)}), f32[16,96,1]{1,2,0:T(1,128)S(1)}, u32[]{:S(2)}, u32[]{:S(2)}) async-start(f32[16,96,1]{1,2,0:T(1,128)} %bitcast.3), calls=%async_computation.2 | async-start | bytes 16384 | tf_op jit(solution)/shard_map/all_to_all | solution.py:59
  86.2 0.0 copy-done
  86.2 0.0 copy-done.3
  86.2 1.4 %fusion.9 = f32[256,512]{1,0:T(8,128)} fusion(bf16[1536,512]{1,0:T(8,128)(2,1)S(1)} %bitcast.9, s32[1536]{0:T(1024)S(1)} %all_to_all.23, f32[256,512]{1,0:T(8,128)S(1)} %copy-done.3, f32[256]{0:T(256)S(1)} %add.67, f32[256]{0:T(256)S(1)} %copy-done.2), kind=kOutput, calls=%fused_computation.19 | convolution fusion | flops 403439616 | bytes 2629632 | tf_op jit(solution)/shard_map/dot_general | solution.py:40
  87.6 5.9 %all-to-all-done.2 = f32[16,96,1]{1,2,0:T(1,128)S(1)} async-done(((f32[16,96,1]{1,2,0:T(1,128)}), f32[16,96,1]{1,2,0:T(1,128)S(1)}, u32[]{:S(2)}, u32[]{:S(2)}) %all-to-all-start.2) | async-done | bytes 6176 | tf_op jit(solution)/shard_map/all_to_all | solution.py:59
  93.4 0.5 broadcast.79
  94.0 0.7 reduce.9
  94.6 0.1 all_to_all.29
  94.7 4.5 %gather_fusion = f32[768]{0:T(1024)S(1)} fusion(f32[1536]{0:T(1024)S(1)} %all_to_all.29, s32[1024]{0:T(1024)S(1)} %pad_clamp_fusion), kind=kCustom, calls=%fused_computation | custom fusion | bytes 9216 | tf_op jit(solution)/shard_map/jit(_take)/gather | solution.py:60
  99.2 0.6 and_select_fusion
  (9 shorter events, 0.1 us)
Async XLA Ops:
  7.2 5.5 %copy-start.1 = (f32[768,512]{1,0:T(8,128)S(1)}, f32[768,512]{1,0:T(8,128)}, u32[]{:S(2)}) copy-start(f32[768,512]{1,0:T(8,128)} %param.4) | copy-start | bytes 4718596
  7.2 67.2 %all-gather.5.cloned.1.call-start = ((), (), s32[]{:S(2)}) async-start(), calls=%async_computation.3 | async-start | bytes 4718592 | tf_op jit(solution)/shard_map/all_gather | solution.py:46
  60.1 14.1 %copy-start.2 = (f32[256]{0:T(256)S(1)}, f32[256]{0:T(256)}, u32[]{:S(2)}) copy-start(f32[256]{0:T(256)} %param.7) | copy-start | bytes 3076
  61.6 11.2 %all-to-all-start = ((s32[16,96,1]{1,2,0:T(1,128)}), s32[16,96,1]{1,2,0:T(1,128)S(1)}, u32[]{:S(2)}, u32[]{:S(2)}) async-start(s32[16,96,1]{1,2,0:T(1,128)} %bitcast), calls=%async_computation | async-start | bytes 16384 | tf_op jit(solution)/shard_map/all_to_all | solution.py:35
  74.4 11.8 %copy-start = (bf16[16,96,512]{2,1,0:T(8,128)(2,1)S(1)}, bf16[16,96,512]{2,1,0:T(8,128)(2,1)}, u32[]{:S(2)}) copy-start(bf16[16,96,512]{2,1,0:T(8,128)(2,1)} %all_to_all.33) | copy-start | bytes 4718596
  74.4 11.8 %copy-start.3 = (f32[256,512]{1,0:T(8,128)S(1)}, f32[256,512]{1,0:T(8,128)}, u32[]{:S(2)}) copy-start(f32[256,512]{1,0:T(8,128)} %param.6) | copy-start | bytes 1572868
  82.7 10.8 %all-to-all-start.2 = ((f32[16,96,1]{1,2,0:T(1,128)}), f32[16,96,1]{1,2,0:T(1,128)S(1)}, u32[]{:S(2)}, u32[]{:S(2)}) async-start(f32[16,96,1]{1,2,0:T(1,128)} %bitcast.3), calls=%async_computation.2 | async-start | bytes 16384 | tf_op jit(solution)/shard_map/all_to_all | solution.py:59
Sparse Core Ops, SparseCore 0:
  60.3 10.4 all-gather.4
